TPU v7x, 32 devices: a whole 2x2x4 slice. The times are simulated.
32 devices in a mesh: seq: 8 (over z, y), head: 4 (over x, core).
Axes of the slice: x: 2, y: 2, z: 4, core: 2. Of those that a mesh axis runs over, the one named last changes fastest.
Arguments:
- q_low: bfloat16 [2048, 1536], P('seq', 'head'), may hold values from -500 to 500
- q_gain: bfloat16 [1536], P('head'), may hold values from 0.099609375 to 1.8984375
- q_up: bfloat16 [1536, 24576], P(None, 'head'), may hold values from -0.15625 to 0.15625
- key_absorb: bfloat16 [128, 128, 512], P('head'), may hold values from -0.5 to 0.5
- value_absorb: bfloat16 [128, 512, 128], P('head'), may hold values from -0.25 to 0.25
- latent_cache: bfloat16 [65536, 576], P('seq'), may hold values from -1300 to 1300
- tile_picks: int32 [16, 16], P('seq'), may hold values from 0 to 511, as said below
Outputs:
- attended: bfloat16 [2048, 16384], P('seq', 'head')
Inputs may be any that keep to these rules, and one draw needn't show every extreme that they name: `tile_picks`: the 16 tiles of one query block differ. Of all tiles that the query blocks of one index of seq select together, at most 8 lie in the cache rows of one index of seq, and exactly 8 in those of some index.
All inputs are finite; a program needn't handle non-finite values.
Results may differ from a plain program's by a relative error of at most 0.03.
Values may be sent and summed in bfloat16 or wider, within the bound.
A program may use at most 192 MiB of HBM per device.

v0:
```python
import jax
import jax.numpy as jnp
from jax import lax
from jax.sharding import PartitionSpec as P

NOPE = 128
ROPE = 64
LATENT = 512
VDIM = 128
TILE = 128
TOPT = 16
QBLK = 128


def rms_normed(q_low, q_gain):
    values = q_low.astype(jnp.float32)
    power = jnp.mean(values * values, axis=-1, keepdims=True)
    return (values * lax.rsqrt(power + 1e-06) * q_gain.astype(jnp.float32)).astype(jnp.bfloat16)


def rotate(rope, positions):
    half = rope.shape[-1] // 2
    freq = jnp.power(
        jnp.float32(10000.0), -(2.0 * jnp.arange(half, dtype=jnp.float32)) / rope.shape[-1]
    )
    angle = positions.astype(jnp.float32)[:, None] * freq[None, :]
    cosine = jnp.cos(angle)[:, None, :]
    sine = jnp.sin(angle)[:, None, :]
    first = rope[..., :half].astype(jnp.float32)
    second = rope[..., half:].astype(jnp.float32)
    return jnp.concatenate(
        [first * cosine - second * sine, first * sine + second * cosine], axis=-1
    ).astype(jnp.bfloat16)


def owner_rank(picks, tiles_dev):
    owner = picks // tiles_dev
    order = jnp.arange(picks.shape[0], dtype=jnp.int32)
    before = (owner[:, None] == owner[None, :]) & (order[None, :] < order[:, None])
    return (owner, jnp.sum(before.astype(jnp.int32), axis=1))


def place_table(place, local, length):
    hit = place[:, None] == jnp.arange(length, dtype=jnp.int32)[None, :]
    return jnp.sum(jnp.where(hit, local[:, None], 0), axis=0)


def body(q_low, q_gain, q_up, key_absorb, value_absorb, latent_cache, tile_picks):
    whole_low, whole_gain = (
        lax.all_gather(q_low, "head", axis=1, tiled=True),
        lax.all_gather(q_gain, "head", axis=0, tiled=True),
    )
    rows = whole_low.shape[0]
    group = key_absorb.shape[0]
    width = latent_cache.shape[1]
    seq_count = lax.axis_size("seq")
    tiles_dev = latent_cache.shape[0] // TILE
    picks = tile_picks.reshape(-1)
    count = picks.shape[0]
    cap = max(2, 2 * count // seq_count)
    owner, rank = owner_rank(picks, tiles_dev)
    cache_tiles = latent_cache.reshape(tiles_dev, TILE, width)
    share = TILE // lax.axis_size("head")
    cache_tiles = lax.dynamic_slice_in_dim(cache_tiles, lax.axis_index("head") * share, share, 1)
    requests = place_table(owner * cap + rank, picks % tiles_dev, seq_count * cap).reshape(
        seq_count, cap
    )
    serve_requests = lax.all_to_all(requests, "seq", split_axis=0, concat_axis=0, tiled=True)
    found = jnp.take(cache_tiles, serve_requests, axis=0)
    fetched = lax.all_to_all(found, "seq", split_axis=0, concat_axis=0, tiled=True)
    flat = fetched.reshape(seq_count * cap, fetched.shape[2], width)
    keys = jnp.take(flat, owner * cap + rank, axis=0)
    keys = lax.all_gather(keys, "head", axis=1, tiled=True)
    keys = keys.reshape(count // TOPT, TOPT * TILE, width)
    normed = rms_normed(whole_low, whole_gain)
    query = jnp.dot(normed, q_up, preferred_element_type=jnp.float32).astype(jnp.bfloat16)
    query = query.reshape(rows, group, NOPE + ROPE)
    context = latent_cache.shape[0] * seq_count
    positions = context + lax.axis_index("seq") * rows + jnp.arange(rows, dtype=jnp.int32)
    rotated = rotate(query[..., NOPE:], positions)
    latent_q = jnp.einsum(
        "thn,hnl->thl", query[..., :NOPE], key_absorb, preferred_element_type=jnp.float32
    ).astype(jnp.bfloat16)
    full_q = jnp.concatenate([latent_q, rotated], axis=-1).reshape(
        count // TOPT, QBLK * group, width
    )
    scale = float(NOPE + ROPE) ** (-0.5)

    def one_block(operands):
        block_q, block_keys = operands
        scores = (
            lax.dot_general(
                block_q, block_keys, (((1,), (1,)), ((), ())), preferred_element_type=jnp.float32
            )
            * scale
        )
        weights = jax.nn.softmax(scores, axis=-1).astype(jnp.bfloat16)
        return jnp.dot(weights, block_keys[:, :LATENT], preferred_element_type=jnp.float32).astype(
            jnp.bfloat16
        )

    mixed = lax.map(one_block, (full_q, keys)).reshape(rows, group, LATENT)
    attended = jnp.einsum("thl,hlv->thv", mixed, value_absorb, preferred_element_type=jnp.float32)
    return attended.astype(jnp.bfloat16).reshape(rows, group * VDIM)


def solution(mesh):
    in_specs = (
        P("seq", "head"),
        P("head"),
        P(None, "head"),
        P("head", None, None),
        P("head", None, None),
        P("seq", None),
        P("seq", None),
    )
    out_specs = P("seq", "head")
    return jax.shard_map(body, mesh=mesh, in_specs=in_specs, out_specs=out_specs, check_vma=False)
```

profile of v0, /device:TPU:0, one launch (start us, length us, event | category | flops | bytes accessed | tf_op | source)
XLA Modules:
  0.0 304.3 jit_solution(13812923504323022759)
XLA Ops:
  6.5 0.8 reshape.301
  7.3 0.2 convert_reduce_fusion
  7.5 0.1 select_reduce_fusion
  7.6 0.7 all_to_all.13
  8.3 7.3 %all-to-all-start = ((s32[8,1,8]{2,1,0:T(1,128)}), s32[8,1,8]{2,1,0:T(1,128)S(1)}, u32[]{:S(2)}, u32[]{:S(2)}) async-start(s32[8,1,8]{2,1,0:T(1,128)} %bitcast.6), calls=%async_computation | async-start | bytes 8192 | tf_op jit(solution)/shard_map/all_to_all | solution.py:68
  15.6 14.1 %copy.49 = bf16[8192,576]{1,0:T(8,128)(2,1)} copy(bf16[8192,576]{0,1:T(8,128)(2,1)} %param.14) | data formatting | bytes 18874368 | tf_op args[5]
  29.7 2.0 constant_dynamic-slice_fusion
  31.6 0.0 all-to-all-done
  31.7 0.1 reshape.310
  31.8 2.4 gather_fusion
  34.1 3.6 %broadcast_select_fusion = bf16[8,8,32,576]{3,2,1,0:T(8,128)(2,1)} fusion(bf16[8,8,32,576]{3,2,1,0:T(8,128)(2,1)} %bitcast.53, pred[8,8]{1,0:T(8,128)(4,1)S(1)} %compare_and_fusion), kind=kLoop, calls=%fused_computation.22 | loop fusion | flops 1179648 | bytes 4718656 | tf_op jit(solution)/shard_map/jit(_take)/select_n | solution.py:69
  37.8 6.1 %all-to-all-start.1 = ((bf16[8,8,32,576]{3,2,1,0:T(8,128)(2,1)}), bf16[8,8,32,576]{3,2,1,0:T(8,128)(2,1)S(1)}, u32[]{:S(2)}, u32[]{:S(2)}) async-start(bf16[8,8,32,576]{3,2,1,0:T(8,128)(2,1)} %broadcast_select_fusion), calls=%async_computation.1 | async-start | bytes 5242880 | tf_op jit(solution)/shard_map/all_to_all | solution.py:70
  43.9 0.0 all-gather.3.cloned.1.call-start
  43.9 0.0 copy-done.5
  43.9 0.1 reshape.304
  44.0 58.8 %all-to-all-done.1 = bf16[8,8,32,576]{3,2,1,0:T(8,128)(2,1)S(1)} async-done(((bf16[8,8,32,576]{3,2,1,0:T(8,128)(2,1)}), bf16[8,8,32,576]{3,2,1,0:T(8,128)(2,1)S(1)}, u32[]{:S(2)}, u32[]{:S(2)}) %all-to-all-start.1) | async-done | bytes 2359328 | tf_op jit(solution)/shard_map/all_to_all | solution.py:70
  102.8 1.8 gather_fusion.1
  104.5 2.6 broadcast_select_fusion.1
  107.2 0.0 all-gather.3.cloned.1.call-update
  107.2 0.0 copy-done.4
  107.2 5.2 %all-gather = bf16[4,1,384]{2,1,0:T(2,128)(2,1)S(1)} all-gather(bf16[1,1,384]{2,1,0:T(2,128)(2,1)S(1)} %reshape.325), channel_id=1, replica_groups=mesh['seq'=8,'head'=4] {'head'}, dimensions={0}, use_global_device_ids=true | all-gather | bytes 3840 | tf_op jit(solution)/shard_map/all_gather | solution.py:51
  112.4 0.0 copy-done.3
  112.4 12.5 %all_gather.9 = bf16[256,1536]{1,0:T(8,128)(2,1)S(1)} all-gather(bf16[256,384]{1,0:T(8,128)(2,1)S(1)} %copy-done.3), channel_id=1, replica_groups=mesh['seq'=8,'head'=4] {'head'}, dimensions={1}, use_global_device_ids=true | all-gather | bytes 983040 | tf_op jit(solution)/shard_map/all_gather | solution.py:50
  124.9 0.2 fusion.17
  125.2 13.1 %convolution_convert_fusion = bf16[256,6144]{1,0:T(8,128)(2,1)} fusion(bf16[1536,6144]{1,0:T(8,128)(2,1)} %param.11, bf16[256,1536]{1,0:T(8,128)(2,1)S(1)} %all_gather.9, f32[1536]{0:T(1024)S(1)} %reshape.327, f32[256]{0:T(256)S(1)} %add_rsqrt_fusion), kind=kOutput, calls=%fused_computation.21 | convolution fusion | flops 4834983936 | bytes 22813696 | tf_op jit(solution)/shard_map/dot_general | solution.py:76
  138.2 3.2 %copy.43 = bf16[256,6144]{0,1:T(8,128)(2,1)S(1)} copy(bf16[256,6144]{1,0:T(8,128)(2,1)} %convolution_convert_fusion) | data formatting | bytes 6291456 | tf_op jit(solution)/shard_map/convert_element_type | solution.py:76
  141.5 0.2 multiply_cosine_fusion
  141.7 1.3 fusion.21
  143.0 2.7 copy.45
  145.7 2.6 copy.46
  148.3 4.8 %convert_bitcast_fusion = bf16[256,32,512]{2,0,1:T(8,128)(2,1)S(1)} fusion(bf16[32,128,512]{2,1,0:T(8,128)(2,1)} %param.12, bf16[256,32,192]{0,2,1:T(8,128)(2,1)S(1)} %bitcast.51), kind=kOutput, calls=%fused_computation.20 | convolution fusion | flops 1077936128 | bytes 14680064 | tf_op jit(solution)/shard_map/thn,hnl->thl/dot_general | solution.py:81
  153.1 0.0 copy-done.1
  153.1 0.0 copy-done.2
  153.1 12.0 %pad_maximum_fusion = bf16[256,32,576]{2,0,1:T(8,128)(2,1)} fusion(bf16[256,32,32]{2,0,1:T(8,128)(2,1)S(1)} %copy-done.2, bf16[256,32,32]{2,0,1:T(8,128)(2,1)S(1)} %copy-done.1, bf16[256,32,512]{2,0,1:T(8,128)(2,1)S(1)} %convert_bitcast_fusion), kind=kLoop, calls=%fused_computation.17 | loop fusion | flops 28311552 | bytes 18874368 | tf_op jit(solution)/shard_map/concatenate | solution.py:84
  165.1 14.0 %copy.47 = bf16[256,32,576]{2,1,0:T(8,128)(2,1)} copy(bf16[256,32,576]{2,0,1:T(8,128)(2,1)} %pad_maximum_fusion) | data formatting | bytes 18874368 | tf_op jit(solution)/shard_map/concatenate | solution.py:84
  179.1 105.8 %while.10 = (s32[]{:T(128)}, bf16[2,4096,512]{2,1,0:T(8,128)(2,1)}, bf16[2,4096,576]{2,1,0:T(8,128)(2,1)}, bf16[2,2048,576]{2,1,0:T(8,128)(2,1)}, s32[]{:T(128)}) while((s32[]{:T(128)}, bf16[2,4096,512]{2,1,0:T(8,128)(2,1)}, bf16[2,4096,576]{2,1,0:T(8,128)(2,1)}, bf16[2,2048,576]{2,1,0:T(8,128)(2,1)}, s32[]{:T(128)}) %tuple.31), condition=%wide.region_6.7_spmd, body=%wide.region_3.6_spmd.sunk | while | flops 18331197440 | bytes 138495600 | solution.py:102
  179.1 22.0 %multiply_reduce_fusion.2 = (f32[4096]{0:T(1024)S(1)}, f32[4096,2048]{0,1:T(8,128)}) fusion(bf16[2,2048,576]{2,1,0:T(8,128)(2,1)} %get-tuple-element.88, s32[]{:T(128)} %get-tuple-element.80, bf16[2,4096,576]{2,1,0:T(8,128)(2,1)} %get-tuple-element.87), kind=kOutput, calls=%fused_computation.4.clone.1 | convolution fusion | flops 9680449536 | bytes 41436160 | tf_op jit(solution)/shard_map/while/body/eval_jaxpr/dot_general | solution.py:92
  201.1 14.0 %fusion.36 = f32[4096]{0:T(1024)S(1)} fusion(f32[4096,2048]{0,1:T(8,128)} %get-tuple-element.73, f32[4096]{0:T(1024)S(1)} %get-tuple-element.74), kind=kLoop, calls=%fused_computation.5.clone.1 | loop fusion | flops 25161728 | bytes 33587200 | tf_op jit(solution)/shard_map/while/body/eval_jaxpr/reduce_sum | solution.py:97
  215.2 0.0 copy-done
  215.2 0.2 dynamic-slice_bitcast_fusion.3
  215.4 16.6 %fusion.37 = bf16[2,4096,512]{2,1,0:T(8,128)(2,1)} fusion(bf16[2,4096,512]{2,1,0:T(8,128)(2,1)} %get-tuple-element.81, s32[]{:T(128)} %get-tuple-element.80, f32[4096,2048]{0,1:T(8,128)} %get-tuple-element.73, f32[4096]{0:T(1024)S(1)} %fusion.36, f32[4096]{0:T(1024)S(1)} %get-tuple-element.74, bf16[2048,576]{1,0:T(8,128)(2,1)S(1)} %dynamic-slice_bitcast_fusion.3), kind=kOutput, calls=%fused_computation.9.clone.1 | convolution fusion | flops 8625586176 | bytes 39879168 | tf_op jit(solution)/shard_map/while/body/eval_jaxpr/dot_general | solution.py:98
  232.0 22.0 %multiply_reduce_fusion.2 = (f32[4096]{0:T(1024)S(1)}, f32[4096,2048]{0,1:T(8,128)}) fusion(bf16[2,2048,576]{2,1,0:T(8,128)(2,1)} %get-tuple-element.88, s32[]{:T(128)} %get-tuple-element.80, bf16[2,4096,576]{2,1,0:T(8,128)(2,1)} %get-tuple-element.87), kind=kOutput, calls=%fused_computation.4.clone.1 | convolution fusion | flops 9680449536 | bytes 41436160 | tf_op jit(solution)/shard_map/while/body/eval_jaxpr/dot_general | solution.py:92
  254.0 14.0 %fusion.36 = f32[4096]{0:T(1024)S(1)} fusion(f32[4096,2048]{0,1:T(8,128)} %get-tuple-element.73, f32[4096]{0:T(1024)S(1)} %get-tuple-element.74), kind=kLoop, calls=%fused_computation.5.clone.1 | loop fusion | flops 25161728 | bytes 33587200 | tf_op jit(solution)/shard_map/while/body/eval_jaxpr/reduce_sum | solution.py:97
  268.1 0.0 copy-done
  268.1 0.2 dynamic-slice_bitcast_fusion.3
  268.3 16.6 %fusion.37 = bf16[2,4096,512]{2,1,0:T(8,128)(2,1)} fusion(bf16[2,4096,512]{2,1,0:T(8,128)(2,1)} %get-tuple-element.81, s32[]{:T(128)} %get-tuple-element.80, f32[4096,2048]{0,1:T(8,128)} %get-tuple-element.73, f32[4096]{0:T(1024)S(1)} %fusion.36, f32[4096]{0:T(1024)S(1)} %get-tuple-element.74, bf16[2048,576]{1,0:T(8,128)(2,1)S(1)} %dynamic-slice_bitcast_fusion.3), kind=kOutput, calls=%fused_computation.9.clone.1 | convolution fusion | flops 8625586176 | bytes 39879168 | tf_op jit(solution)/shard_map/while/body/eval_jaxpr/dot_general | solution.py:98
  284.9 9.7 %fusion.14 = bf16[32,256,128]{1,2,0:T(8,128)(2,1)S(1)} fusion(bf16[32,512,128]{2,1,0:T(8,128)(2,1)} %param.13, bf16[256,32,512]{2,1,0:T(8,128)(2,1)} %bitcast.58), kind=kOutput, calls=%fused_computation.26 | convolution fusion | flops 1074790400 | bytes 14680064 | tf_op jit(solution)/shard_map/thl,hlv->thv/dot_general | solution.py:103
  294.6 2.9 copy.52
  (22 shorter events, 0.2 us)
Async XLA Ops:
  8.3 23.4 %all-to-all-start = ((s32[8,1,8]{2,1,0:T(1,128)}), s32[8,1,8]{2,1,0:T(1,128)S(1)}, u32[]{:S(2)}, u32[]{:S(2)}) async-start(s32[8,1,8]{2,1,0:T(1,128)} %bitcast.6), calls=%async_computation | async-start | bytes 8192 | tf_op jit(solution)/shard_map/all_to_all | solution.py:68
  34.1 9.8 %copy-start.5 = (s32[2,16]{1,0:T(2,128)S(1)}, s32[2,16]{1,0:T(2,128)}, u32[]{:S(2)}) copy-start(s32[2,16]{1,0:T(2,128)} %param.15) | copy-start | bytes 388
  37.7 69.4 %copy-start.4 = (bf16[384]{0:T(512)(128)(2,1)S(1)}, bf16[384]{0:T(512)(128)(2,1)}, u32[]{:S(2)}) copy-start(bf16[384]{0:T(512)(128)(2,1)} %param.10) | copy-start | bytes 2308
  37.8 74.7 %copy-start.3 = (bf16[256,384]{1,0:T(8,128)(2,1)S(1)}, bf16[256,384]{1,0:T(8,128)(2,1)}, u32[]{:S(2)}) copy-start(bf16[256,384]{1,0:T(8,128)(2,1)} %param.9) | copy-start | bytes 589828
  37.8 65.0 %all-to-all-start.1 = ((bf16[8,8,32,576]{3,2,1,0:T(8,128)(2,1)}), bf16[8,8,32,576]{3,2,1,0:T(8,128)(2,1)S(1)}, u32[]{:S(2)}, u32[]{:S(2)}) async-start(bf16[8,8,32,576]{3,2,1,0:T(8,128)(2,1)} %broadcast_select_fusion), calls=%async_computation.1 | async-start | bytes 5242880 | tf_op jit(solution)/shard_map/all_to_all | solution.py:70
  43.9 135.3 %all-gather.3.cloned.1.call-start = ((), (), s32[]{:S(2)}) async-start(), calls=%async_computation.2 | async-start | bytes 6553600 | tf_op jit(solution)/shard_map/all_gather | solution.py:73
  148.3 4.8 %copy-start.1 = (bf16[256,32,32]{2,0,1:T(8,128)(2,1)S(1)}, bf16[256,32,32]{2,0,1:T(8,128)(2,1)}, u32[]{:S(2)}) copy-start(bf16[256,32,32]{2,0,1:T(8,128)(2,1)} %copy.45) | copy-start | bytes 1572868
  148.3 4.8 %copy-start.2 = (bf16[256,32,32]{2,0,1:T(8,128)(2,1)S(1)}, bf16[256,32,32]{2,0,1:T(8,128)(2,1)}, u32[]{:S(2)}) copy-start(bf16[256,32,32]{2,0,1:T(8,128)(2,1)} %copy.46) | copy-start | bytes 1572868
  201.1 14.0 %copy-start = (bf16[2,2048,576]{2,1,0:T(8,128)(2,1)S(1)}, bf16[2,2048,576]{2,1,0:T(8,128)(2,1)}, u32[]{:S(2)}) copy-start(bf16[2,2048,576]{2,1,0:T(8,128)(2,1)} %get-tuple-element.88) | copy-start | bytes 14155780 | tf_op jit(solution)/shard_map/while
  254.0 14.0 %copy-start = (bf16[2,2048,576]{2,1,0:T(8,128)(2,1)S(1)}, bf16[2,2048,576]{2,1,0:T(8,128)(2,1)}, u32[]{:S(2)}) copy-start(bf16[2,2048,576]{2,1,0:T(8,128)(2,1)} %get-tuple-element.88) | copy-start | bytes 14155780 | tf_op jit(solution)/shard_map/while
Sparse Core Ops, SparseCore 0:
  107.3 42.6 all-gather.2
where the time goes:
time: 305 us; the launch traced here: 304 us
  matrix products  105 us (34%)
  waiting for transfers between devices  58.8 us (19%)
  other arithmetic  48.4 us (16%)
  local copies, waits for them, and re-layouts  47.7 us (16%)
  blocking collectives  17.7 us (6%)
  starting transfers between devices  13.5 us (4%)
  between operations  13.5 us (4%)
    all_to_all x1, waiting for transfers between devices, body(): lax.all_to_all(found, 'seq', split_axis=0, concat_axis=0, tiled=True)  58.8 us
    dot_general x2, matrix products, one_block(): lax.dot_general(block_q, block_keys, (((1,), (1,)), ((), ())), preferred_...  44 us
    dot_general x2, matrix products, one_block(): jnp.dot(weights, block_keys[:, :LATENT], preferred_element_type=jnp.float32)  33.2 us
    reduce_sum x2, other arithmetic, one_block(): weights = jax.nn.softmax(scores, axis=-1).astype(jnp.bfloat16)  28 us
    unnamed x12, local copies, waits for them, and re-layouts  14.1 us
    concatenate x1, local copies, waits for them, and re-layouts, body(): jnp.concatenate([latent_q, rotated], axis=-1)  14 us
    dot_general x1, matrix products, body(): jnp.dot(normed, q_up, preferred_element_type=jnp.float32)  13.1 us
    all_gather x1, blocking collectives, body(): lax.all_gather(q_low, 'head', axis=1, tiled=True)  12.5 us
  transfers between devices with their start and end apart: 3, of which 1 were waited for; matrix products, arithmetic and copies ran while one was open for 23% of the time, Pallas kernels for 0%

commit v1 on v0

--- a/solution.py
+++ b/solution.py
@@ -2,6 +2,7 @@
 import jax.numpy as jnp
 from jax import lax
 from jax.sharding import PartitionSpec as P
+from jax.lax import axis_index, axis_size, ppermute
 
 NOPE = 128
 ROPE = 64
@@ -67,7 +68,23 @@
     )
     serve_requests = lax.all_to_all(requests, "seq", split_axis=0, concat_axis=0, tiled=True)
     found = jnp.take(cache_tiles, serve_requests, axis=0)
-    fetched = lax.all_to_all(found, "seq", split_axis=0, concat_axis=0, tiled=True)
+    reached = axis_size("seq")
+    p_next = axis_index("seq")
+    moved, everything = (reached, p_next)
+    y2 = found.shape[0] // moved
+    oldest = list(found.shape)
+    oldest[0] = y2
+    met_up = oldest[0]
+    oldest[0] = met_up * moved
+    fetched = jnp.zeros(oldest, found.dtype)
+    for dd in tuple(range(moved)):
+        back = lax.dynamic_slice_in_dim(found, (everything ^ dd) * y2, y2, axis=0)
+        if dd:
+            shelf = []
+            for src_i in [*range(moved)]:
+                shelf.append((src_i, src_i ^ dd))
+            back = ppermute(back, "seq", shelf)
+        fetched = lax.dynamic_update_slice_in_dim(fetched, back, (everything ^ dd) * met_up, axis=0)
     flat = fetched.reshape(seq_count * cap, fetched.shape[2], width)
     keys = jnp.take(flat, owner * cap + rank, axis=0)
     keys = lax.all_gather(keys, "head", axis=1, tiled=True)

time: 305 us -> 302 us (level)
  the two profiles are of different devices: /device:TPU:0 before, /device:TPU:19 now
where the time goes in v1:
time: 302 us; the launch traced here: 301 us
  matrix products  105 us (35%)
  waiting for transfers between devices  54.4 us (18%)
  local copies, waits for them, and re-layouts  48.6 us (16%)
  other arithmetic  46.8 us (15%)
  blocking collectives  21.1 us (7%)
  between operations  13.6 us (5%)
  starting transfers between devices  11.9 us (4%)
    ppermute x7, waiting for transfers between devices, body(): back = ppermute(back, 'seq', shelf)  54.4 us
    dot_general x2, matrix products, one_block(): lax.dot_general(block_q, block_keys, (((1,), (1,)), ((), ())), preferred_...  44 us
    dot_general x2, matrix products, one_block(): jnp.dot(weights, block_keys[:, :LATENT], preferred_element_type=jnp.float32)  33.3 us
    reduce_sum x2, other arithmetic, one_block(): weights = jax.nn.softmax(scores, axis=-1).astype(jnp.bfloat16)  28 us
    unnamed x12, local copies, waits for them, and re-layouts  14.1 us
    concatenate x1, local copies, waits for them, and re-layouts, body(): jnp.concatenate([latent_q, rotated], axis=-1)  14 us
    all_gather x1, blocking collectives, body(): lax.all_gather(q_low, 'head', axis=1, tiled=True)  13.2 us
    dot_general x1, matrix products, body(): jnp.dot(normed, q_up, preferred_element_type=jnp.float32)  13.2 us
  transfers between devices with their start and end apart: 9, of which 6 were waited for; matrix products, arithmetic and copies ran while one was open for 23% of the time, Pallas kernels for 0%

profile of v1, /device:TPU:19, one launch (start us, length us, event | category | flops | bytes accessed | tf_op | source)
XLA Modules:
  0.0 301.4 jit_solution(4606635840186000333)
XLA Ops:
  6.5 0.8 reshape.301
  7.3 0.2 convert_reduce_fusion
  7.5 0.1 select_reduce_fusion
  7.6 0.7 all_to_all.10
  8.3 5.6 %all-to-all-start = ((s32[8,1,8]{2,1,0:T(1,128)}), s32[8,1,8]{2,1,0:T(1,128)S(1)}, u32[]{:S(2)}, u32[]{:S(2)}) async-start(s32[8,1,8]{2,1,0:T(1,128)} %bitcast.6), calls=%async_computation | async-start | bytes 8192 | tf_op jit(solution)/shard_map/all_to_all | solution.py:69
  13.9 14.0 %copy.49 = bf16[8192,576]{1,0:T(8,128)(2,1)} copy(bf16[8192,576]{0,1:T(8,128)(2,1)} %param.14) | data formatting | bytes 18874368 | tf_op args[5]
  27.9 2.0 constant_dynamic-slice_fusion.7
  30.1 2.4 gather_fusion
  32.5 2.1 broadcast_select_fusion
  34.6 0.3 broadcast_in_dim.59
  34.9 0.4 constant_dynamic-slice_fusion
  35.2 1.2 collective-permute-start
  36.5 1.2 collective-permute-start.1
  37.7 0.3 collective-permute-start.2
  38.0 0.1 collective-permute-start.3
  38.1 3.2 %collective-permute-start.4 = (bf16[1,8,32,576]{3,2,1,0:T(8,128)(2,1)S(1)}, bf16[1,8,32,576]{3,2,1,0:T(8,128)(2,1)S(1)}, u32[]{:S(2)}, u32[]{:S(2)}) collective-permute-start(bf16[1,8,32,576]{3,2,1,0:T(8,128)(2,1)S(1)} %get-tuple-element.44), channel_id=1, source_target_pairs={{0,20},{4,16},{8,28},{12,24},{16,4},{20,0},{24,12},{28,8},{1,21},{... | collective-permute-start | bytes 884744 | tf_op jit(solution)/shard_map/ppermute | solution.py:86
  41.3 2.0 collective-permute-done
  43.3 0.3 collective-permute-start.5
  43.7 11.0 %collective-permute-done.1 = bf16[1,8,32,576]{3,2,1,0:T(8,128)(2,1)S(1)} collective-permute-done((bf16[1,8,32,576]{3,2,1,0:T(8,128)(2,1)S(1)}, bf16[1,8,32,576]{3,2,1,0:T(8,128)(2,1)S(1)}, u32[]{:S(2)}, u32[]{:S(2)}) %collective-permute-start.1) | collective-permute-done | bytes 294944 | tf_op jit(solution)/shard_map/ppermute | solution.py:86
  54.7 7.1 %collective-permute-done.2 = bf16[1,8,32,576]{3,2,1,0:T(8,128)(2,1)S(1)} collective-permute-done((bf16[1,8,32,576]{3,2,1,0:T(8,128)(2,1)S(1)}, bf16[1,8,32,576]{3,2,1,0:T(8,128)(2,1)S(1)}, u32[]{:S(2)}, u32[]{:S(2)}) %collective-permute-start.2) | collective-permute-done | bytes 294944 | tf_op jit(solution)/shard_map/ppermute | solution.py:86
  61.9 3.4 %collective-permute-done.4 = bf16[1,8,32,576]{3,2,1,0:T(8,128)(2,1)S(1)} collective-permute-done((bf16[1,8,32,576]{3,2,1,0:T(8,128)(2,1)S(1)}, bf16[1,8,32,576]{3,2,1,0:T(8,128)(2,1)S(1)}, u32[]{:S(2)}, u32[]{:S(2)}) %collective-permute-start.4) | collective-permute-done | bytes 294944 | tf_op jit(solution)/shard_map/ppermute | solution.py:86
  65.4 23.0 %collective-permute-done.5 = bf16[1,8,32,576]{3,2,1,0:T(8,128)(2,1)S(1)} collective-permute-done((bf16[1,8,32,576]{3,2,1,0:T(8,128)(2,1)S(1)}, bf16[1,8,32,576]{3,2,1,0:T(8,128)(2,1)S(1)}, u32[]{:S(2)}, u32[]{:S(2)}) %collective-permute-start.5) | collective-permute-done | bytes 294944 | tf_op jit(solution)/shard_map/ppermute | solution.py:86
  88.4 7.9 %collective-permute-done.6 = bf16[1,8,32,576]{3,2,1,0:T(8,128)(2,1)S(1)} collective-permute-done((bf16[1,8,32,576]{3,2,1,0:T(8,128)(2,1)S(1)}, bf16[1,8,32,576]{3,2,1,0:T(8,128)(2,1)S(1)}, u32[]{:S(2)}, u32[]{:S(2)}) %collective-permute-start.6) | collective-permute-done | bytes 294944 | tf_op jit(solution)/shard_map/ppermute | solution.py:86
  96.3 1.8 gather_fusion.1
  98.1 2.6 broadcast_select_fusion.1
  100.7 7.9 %all-gather = bf16[4,1,384]{2,1,0:T(2,128)(2,1)S(1)} all-gather(bf16[1,1,384]{2,1,0:T(2,128)(2,1)S(1)} %reshape.325), channel_id=1, replica_groups=mesh['seq'=8,'head'=4] {'head'}, dimensions={0}, use_global_device_ids=true | all-gather | bytes 3840 | tf_op jit(solution)/shard_map/all_gather | solution.py:52
  108.7 13.2 %all_gather.9 = bf16[256,1536]{1,0:T(8,128)(2,1)S(1)} all-gather(bf16[256,384]{1,0:T(8,128)(2,1)S(1)} %copy-done.3), channel_id=1, replica_groups=mesh['seq'=8,'head'=4] {'head'}, dimensions={1}, use_global_device_ids=true | all-gather | bytes 983040 | tf_op jit(solution)/shard_map/all_gather | solution.py:51
  121.9 0.2 fusion.17
  122.2 13.2 %convolution_convert_fusion = bf16[256,6144]{1,0:T(8,128)(2,1)} fusion(bf16[1536,6144]{1,0:T(8,128)(2,1)} %param.11, bf16[256,1536]{1,0:T(8,128)(2,1)S(1)} %all_gather.9, f32[1536]{0:T(1024)S(1)} %reshape.327, f32[256]{0:T(256)S(1)} %add_rsqrt_fusion), kind=kOutput, calls=%fused_computation.21 | convolution fusion | flops 4834983936 | bytes 22813696 | tf_op jit(solution)/shard_map/dot_general | solution.py:93
  135.3 3.2 %copy.43 = bf16[256,6144]{0,1:T(8,128)(2,1)S(1)} copy(bf16[256,6144]{1,0:T(8,128)(2,1)} %convolution_convert_fusion) | data formatting | bytes 6291456 | tf_op jit(solution)/shard_map/convert_element_type | solution.py:93
  138.5 0.2 multiply_cosine_fusion
  138.7 1.3 fusion.21
  140.0 2.7 copy.45
  142.7 2.6 copy.46
  145.4 4.7 %convert_bitcast_fusion = bf16[256,32,512]{2,0,1:T(8,128)(2,1)S(1)} fusion(bf16[32,128,512]{2,1,0:T(8,128)(2,1)} %param.12, bf16[256,32,192]{0,2,1:T(8,128)(2,1)S(1)} %bitcast.51), kind=kOutput, calls=%fused_computation.20 | convolution fusion | flops 1077936128 | bytes 14680064 | tf_op jit(solution)/shard_map/thn,hnl->thl/dot_general | solution.py:98
  150.1 12.0 %pad_maximum_fusion = bf16[256,32,576]{2,0,1:T(8,128)(2,1)} fusion(bf16[256,32,32]{2,0,1:T(8,128)(2,1)S(1)} %copy-done.2, bf16[256,32,32]{2,0,1:T(8,128)(2,1)S(1)} %copy-done.1, bf16[256,32,512]{2,0,1:T(8,128)(2,1)S(1)} %convert_bitcast_fusion), kind=kLoop, calls=%fused_computation.17 | loop fusion | flops 28311552 | bytes 18874368 | tf_op jit(solution)/shard_map/concatenate | solution.py:101
  162.1 14.0 %copy.47 = bf16[256,32,576]{2,1,0:T(8,128)(2,1)} copy(bf16[256,32,576]{2,0,1:T(8,128)(2,1)} %pad_maximum_fusion) | data formatting | bytes 18874368 | tf_op jit(solution)/shard_map/concatenate | solution.py:101
  176.1 105.9 %while.10 = (s32[]{:T(128)}, bf16[2,4096,512]{2,1,0:T(8,128)(2,1)}, bf16[2,4096,576]{2,1,0:T(8,128)(2,1)}, bf16[2,2048,576]{2,1,0:T(8,128)(2,1)}, s32[]{:T(128)}) while((s32[]{:T(128)}, bf16[2,4096,512]{2,1,0:T(8,128)(2,1)}, bf16[2,4096,576]{2,1,0:T(8,128)(2,1)}, bf16[2,2048,576]{2,1,0:T(8,128)(2,1)}, s32[]{:T(128)}) %tuple.38), condition=%wide.region_6.7_spmd, body=%wide.region_3.6_spmd.sunk | while | flops 18331197440 | bytes 138495600 | solution.py:119
  176.1 22.0 %multiply_reduce_fusion.2 = (f32[4096]{0:T(1024)S(1)}, f32[4096,2048]{0,1:T(8,128)}) fusion(bf16[2,2048,576]{2,1,0:T(8,128)(2,1)} %get-tuple-element.96, s32[]{:T(128)} %get-tuple-element.88, bf16[2,4096,576]{2,1,0:T(8,128)(2,1)} %get-tuple-element.95), kind=kOutput, calls=%fused_computation.4.clone.1 | convolution fusion | flops 9680449536 | bytes 41436160 | tf_op jit(solution)/shard_map/while/body/eval_jaxpr/dot_general | solution.py:109
  198.1 14.0 %fusion.36 = f32[4096]{0:T(1024)S(1)} fusion(f32[4096,2048]{0,1:T(8,128)} %get-tuple-element.81, f32[4096]{0:T(1024)S(1)} %get-tuple-element.82), kind=kLoop, calls=%fused_computation.5.clone.1 | loop fusion | flops 25161728 | bytes 33587200 | tf_op jit(solution)/shard_map/while/body/eval_jaxpr/reduce_sum | solution.py:114
  212.1 0.2 dynamic-slice_bitcast_fusion.3
  212.4 16.6 %fusion.37 = bf16[2,4096,512]{2,1,0:T(8,128)(2,1)} fusion(bf16[2,4096,512]{2,1,0:T(8,128)(2,1)} %get-tuple-element.89, s32[]{:T(128)} %get-tuple-element.88, f32[4096,2048]{0,1:T(8,128)} %get-tuple-element.81, f32[4096]{0:T(1024)S(1)} %fusion.36, f32[4096]{0:T(1024)S(1)} %get-tuple-element.82, bf16[2048,576]{1,0:T(8,128)(2,1)S(1)} %dynamic-slice_bitcast_fusion.3), kind=kOutput, calls=%fused_computation.9.clone.1 | convolution fusion | flops 8625586176 | bytes 39879168 | tf_op jit(solution)/shard_map/while/body/eval_jaxpr/dot_general | solution.py:115
  229.0 22.0 %multiply_reduce_fusion.2 = (f32[4096]{0:T(1024)S(1)}, f32[4096,2048]{0,1:T(8,128)}) fusion(bf16[2,2048,576]{2,1,0:T(8,128)(2,1)} %get-tuple-element.96, s32[]{:T(128)} %get-tuple-element.88, bf16[2,4096,576]{2,1,0:T(8,128)(2,1)} %get-tuple-element.95), kind=kOutput, calls=%fused_computation.4.clone.1 | convolution fusion | flops 9680449536 | bytes 41436160 | tf_op jit(solution)/shard_map/while/body/eval_jaxpr/dot_general | solution.py:109
  251.0 14.0 %fusion.36 = f32[4096]{0:T(1024)S(1)} fusion(f32[4096,2048]{0,1:T(8,128)} %get-tuple-element.81, f32[4096]{0:T(1024)S(1)} %get-tuple-element.82), kind=kLoop, calls=%fused_computation.5.clone.1 | loop fusion | flops 25161728 | bytes 33587200 | tf_op jit(solution)/shard_map/while/body/eval_jaxpr/reduce_sum | solution.py:114
  265.1 0.2 dynamic-slice_bitcast_fusion.3
  265.3 16.6 %fusion.37 = bf16[2,4096,512]{2,1,0:T(8,128)(2,1)} fusion(bf16[2,4096,512]{2,1,0:T(8,128)(2,1)} %get-tuple-element.89, s32[]{:T(128)} %get-tuple-element.88, f32[4096,2048]{0,1:T(8,128)} %get-tuple-element.81, f32[4096]{0:T(1024)S(1)} %fusion.36, f32[4096]{0:T(1024)S(1)} %get-tuple-element.82, bf16[2048,576]{1,0:T(8,128)(2,1)S(1)} %dynamic-slice_bitcast_fusion.3), kind=kOutput, calls=%fused_computation.9.clone.1 | convolution fusion | flops 8625586176 | bytes 39879168 | tf_op jit(solution)/shard_map/while/body/eval_jaxpr/dot_general | solution.py:115
  281.9 9.7 %fusion.14 = bf16[32,256,128]{1,2,0:T(8,128)(2,1)S(1)} fusion(bf16[32,512,128]{2,1,0:T(8,128)(2,1)} %param.13, bf16[256,32,512]{2,1,0:T(8,128)(2,1)} %bitcast.58), kind=kOutput, calls=%fused_computation.26 | convolution fusion | flops 1074790400 | bytes 14680064 | tf_op jit(solution)/shard_map/thl,hlv->thv/dot_general | solution.py:120
  291.6 2.9 copy.52
  (43 shorter events, 0.6 us)
Async XLA Ops:
  8.3 21.7 %all-to-all-start = ((s32[8,1,8]{2,1,0:T(1,128)}), s32[8,1,8]{2,1,0:T(1,128)S(1)}, u32[]{:S(2)}, u32[]{:S(2)}) async-start(s32[8,1,8]{2,1,0:T(1,128)} %bitcast.6), calls=%async_computation | async-start | bytes 8192 | tf_op jit(solution)/shard_map/all_to_all | solution.py:69
  13.9 162.2 %all-gather.3.cloned.1.call-start = ((), (), s32[]{:S(2)}) async-start(), calls=%async_computation.1 | async-start | bytes 6553600 | tf_op jit(solution)/shard_map/all_gather | solution.py:90
  27.9 2.0 copy-start.5
  35.2 8.1 %collective-permute-start = (bf16[1,8,32,576]{3,2,1,0:T(8,128)(2,1)S(1)}, bf16[1,8,32,576]{3,2,1,0:T(8,128)(2,1)S(1)}, u32[]{:S(2)}, u32[]{:S(2)}) collective-permute-start(bf16[1,8,32,576]{3,2,1,0:T(8,128)(2,1)S(1)} %get-tuple-element.48), channel_id=1, source_target_pairs={{0,4},{4,0},{8,12},{12,8},{16,20},{20,16},{24,28},{28,24},{1,5},{5... | collective-permute-start | bytes 884744 | tf_op jit(solution)/shard_map/ppermute | solution.py:86
  36.5 18.2 %collective-permute-start.1 = (bf16[1,8,32,576]{3,2,1,0:T(8,128)(2,1)S(1)}, bf16[1,8,32,576]{3,2,1,0:T(8,128)(2,1)S(1)}, u32[]{:S(2)}, u32[]{:S(2)}) collective-permute-start(bf16[1,8,32,576]{3,2,1,0:T(8,128)(2,1)S(1)} %get-tuple-element.47), channel_id=1, source_target_pairs={{0,8},{4,12},{8,0},{12,4},{16,24},{20,28},{24,16},{28,20},{1,9},{5... | collective-permute-start | bytes 884744 | tf_op jit(solution)/shard_map/ppermute | solution.py:86
  37.7 24.2 %collective-permute-start.2 = (bf16[1,8,32,576]{3,2,1,0:T(8,128)(2,1)S(1)}, bf16[1,8,32,576]{3,2,1,0:T(8,128)(2,1)S(1)}, u32[]{:S(2)}, u32[]{:S(2)}) collective-permute-start(bf16[1,8,32,576]{3,2,1,0:T(8,128)(2,1)S(1)} %get-tuple-element.46), channel_id=1, source_target_pairs={{0,12},{4,8},{8,4},{12,0},{16,28},{20,24},{24,20},{28,16},{1,13},{... | collective-permute-start | bytes 884744 | tf_op jit(solution)/shard_map/ppermute | solution.py:86
  38.0 23.9 %collective-permute-start.3 = (bf16[1,8,32,576]{3,2,1,0:T(8,128)(2,1)S(1)}, bf16[1,8,32,576]{3,2,1,0:T(8,128)(2,1)S(1)}, u32[]{:S(2)}, u32[]{:S(2)}) collective-permute-start(bf16[1,8,32,576]{3,2,1,0:T(8,128)(2,1)S(1)} %get-tuple-element.45), channel_id=1, source_target_pairs={{0,16},{4,20},{8,24},{12,28},{16,0},{20,4},{24,8},{28,12},{1,17},{... | collective-permute-start | bytes 884744 | tf_op jit(solution)/shard_map/ppermute | solution.py:86
  38.1 27.2 %collective-permute-start.4 = (bf16[1,8,32,576]{3,2,1,0:T(8,128)(2,1)S(1)}, bf16[1,8,32,576]{3,2,1,0:T(8,128)(2,1)S(1)}, u32[]{:S(2)}, u32[]{:S(2)}) collective-permute-start(bf16[1,8,32,576]{3,2,1,0:T(8,128)(2,1)S(1)} %get-tuple-element.44), channel_id=1, source_target_pairs={{0,20},{4,16},{8,28},{12,24},{16,4},{20,0},{24,12},{28,8},{1,21},{... | collective-permute-start | bytes 884744 | tf_op jit(solution)/shard_map/ppermute | solution.py:86
  43.3 45.0 %collective-permute-start.5 = (bf16[1,8,32,576]{3,2,1,0:T(8,128)(2,1)S(1)}, bf16[1,8,32,576]{3,2,1,0:T(8,128)(2,1)S(1)}, u32[]{:S(2)}, u32[]{:S(2)}) collective-permute-start(bf16[1,8,32,576]{3,2,1,0:T(8,128)(2,1)S(1)} %get-tuple-element.43), channel_id=1, source_target_pairs={{0,24},{4,28},{8,16},{12,20},{16,8},{20,12},{24,0},{28,4},{1,25},{... | collective-permute-start | bytes 884744 | tf_op jit(solution)/shard_map/ppermute | solution.py:86
  54.7 41.6 %collective-permute-start.6 = (bf16[1,8,32,576]{3,2,1,0:T(8,128)(2,1)S(1)}, bf16[1,8,32,576]{3,2,1,0:T(8,128)(2,1)S(1)}, u32[]{:S(2)}, u32[]{:S(2)}) collective-permute-start(bf16[1,8,32,576]{3,2,1,0:T(8,128)(2,1)S(1)} %get-tuple-element.42), channel_id=1, source_target_pairs={{0,28},{4,24},{8,20},{12,16},{16,12},{20,8},{24,4},{28,0},{1,29},{... | collective-permute-start | bytes 884744 | tf_op jit(solution)/shard_map/ppermute | solution.py:86
  96.3 4.4 %copy-start.4 = (bf16[384]{0:T(512)(128)(2,1)S(1)}, bf16[384]{0:T(512)(128)(2,1)}, u32[]{:S(2)}) copy-start(bf16[384]{0:T(512)(128)(2,1)} %param.10) | copy-start | bytes 2308
  96.3 12.4 %copy-start.3 = (bf16[256,384]{1,0:T(8,128)(2,1)S(1)}, bf16[256,384]{1,0:T(8,128)(2,1)}, u32[]{:S(2)}) copy-start(bf16[256,384]{1,0:T(8,128)(2,1)} %param.9) | copy-start | bytes 589828
  145.4 4.7 %copy-start.1 = (bf16[256,32,32]{2,0,1:T(8,128)(2,1)S(1)}, bf16[256,32,32]{2,0,1:T(8,128)(2,1)}, u32[]{:S(2)}) copy-start(bf16[256,32,32]{2,0,1:T(8,128)(2,1)} %copy.45) | copy-start | bytes 1572868
  145.4 4.7 %copy-start.2 = (bf16[256,32,32]{2,0,1:T(8,128)(2,1)S(1)}, bf16[256,32,32]{2,0,1:T(8,128)(2,1)}, u32[]{:S(2)}) copy-start(bf16[256,32,32]{2,0,1:T(8,128)(2,1)} %copy.46) | copy-start | bytes 1572868
  198.1 14.0 %copy-start = (bf16[2,2048,576]{2,1,0:T(8,128)(2,1)S(1)}, bf16[2,2048,576]{2,1,0:T(8,128)(2,1)}, u32[]{:S(2)}) copy-start(bf16[2,2048,576]{2,1,0:T(8,128)(2,1)} %get-tuple-element.96) | copy-start | bytes 14155780 | tf_op jit(solution)/shard_map/while
  251.0 14.0 %copy-start = (bf16[2,2048,576]{2,1,0:T(8,128)(2,1)S(1)}, bf16[2,2048,576]{2,1,0:T(8,128)(2,1)}, u32[]{:S(2)}) copy-start(bf16[2,2048,576]{2,1,0:T(8,128)(2,1)} %get-tuple-element.96) | copy-start | bytes 14155780 | tf_op jit(solution)/shard_map/while
Sparse Core Ops, SparseCore 0:
  100.8 45.3 all-gather.2
